TPU v7x, 32 devices: a whole 2x2x4 slice. The times are simulated.
32 devices in a mesh: member: 2 (over y), seq: 4 (over z), head: 2 (over x), rep: 2 (over core).
Axes of the slice: x: 2, y: 2, z: 4, core: 2. Of those that a mesh axis runs over, the one named last changes fastest.
Arguments:
- x_raw: bfloat16 [4, 4096, 2560], P(('member', 'rep'), 'seq', 'head'), parts along dimension 0, may hold values from -6 to 6
- bc_raw: bfloat16 [4, 4096, 256], P(('member', 'rep'), 'seq'), parts along dimension 0, may hold values from -3 to 3
- gate_in: bfloat16 [4, 4096, 2560], P(('member', 'rep'), 'seq', 'head'), parts along dimension 0, may hold values from -570 to 570
- step_raw: float32 [4, 4096, 40], P(('member', 'rep'), 'seq', 'head'), parts along dimension 0, may hold values from -1.9 to 4.9
- conv_x_weight: bfloat16 [8, 2560], P('member', 'head'), parts along dimension 0, may hold values from -3 to 3
- conv_x_bias: bfloat16 [5120], P(('member', 'head')), parts along dimension 0, may hold values from -0.5 to 0.5
- conv_bc_weight: bfloat16 [8, 256], P('member'), parts along dimension 0, may hold values from -3 to 3
- conv_bc_bias: bfloat16 [512], P('member'), parts along dimension 0, may hold values from -0.5 to 0.5
- dt_bias: float32 [80], P(('member', 'head')), parts along dimension 0, may hold values from -3.5 to 0.55
- a_log: float32 [80], P(('member', 'head')), parts along dimension 0
- d_skip: float32 [80], P(('member', 'head')), parts along dimension 0, may hold values from 0.5 to 2
- norm_gain: float32 [5120], P(('member', 'head')), parts along dimension 0, may hold values from 0.5 to 1.5
Outputs:
- mixer_out: bfloat16 [4, 4096, 2560], P(('member', 'rep'), 'seq', 'head'), parts along dimension 0
There are 2 independent parts, one for each index of `member`. A program takes and returns all parts, laid end to end along the dimension named above; each array names one. Nothing has to cross between parts.
All inputs are finite; a program needn't handle non-finite values.
Results may differ from a plain program's by a relative error of at most 0.0082.
Values may be sent and summed in bfloat16 or wider, within the bound.
A program may use at most 64 MiB of HBM per device.

v0:
```python
import jax
import jax.numpy as jnp
from jax import lax
from jax.sharding import PartitionSpec as P

HEADDIM = 64
STATE = 128
GROUP = 256
CONV = 4
DI = 2560


norm_eps = 1e-05


def passed_along(value, axis, by):
    size = lax.axis_size(axis)
    pairs = [(i, i + by) for i in range(size) if 0 <= i + by < size]
    return lax.ppermute(value, axis, pairs)


def shard_conv(extended, conv_weight, conv_bias, row_count):
    summed = jnp.zeros(
        (extended.shape[0], row_count, extended.shape[2]), jnp.float32
    ) + conv_bias.astype(jnp.float32)
    for tap_index in range(CONV):
        summed = summed + conv_weight[tap_index].astype(jnp.float32) * extended[
            :, tap_index : tap_index + row_count
        ].astype(jnp.float32)
    return jax.nn.silu(summed).astype(jnp.bfloat16)


def entry_boundary(device_decay, device_state, zero_state):

    def relay_turn(turn_index, incoming):
        outgoing = device_decay[:, None, None] * incoming + device_state
        return passed_along(outgoing, "seq", 1)

    return lax.fori_loop(0, lax.axis_size("seq") - 1, relay_turn, zero_state)


def on_device(
    x_raw,
    bc_raw,
    gate_in,
    step_raw,
    conv_x_weight,
    conv_x_bias,
    conv_bc_weight,
    conv_bc_bias,
    dt_bias,
    a_log,
    d_skip,
    norm_gain,
):
    local_len = x_raw.shape[1]
    feat_local = x_raw.shape[2]
    heads_local = dt_bias.shape[0]
    rim_rows = jnp.concatenate(
        (x_raw[:, local_len - CONV + 1 :, :], bc_raw[:, local_len - CONV + 1 :, :]), axis=2
    )
    before = passed_along(rim_rows, "seq", 1)
    x_conv = shard_conv(
        jnp.concatenate((before[:, :, :feat_local], x_raw), axis=1),
        conv_x_weight,
        conv_x_bias,
        local_len,
    )
    bc_conv = shard_conv(
        jnp.concatenate((before[:, :, feat_local:], bc_raw), axis=1),
        conv_bc_weight,
        conv_bc_bias,
        local_len,
    )
    step_size = jax.nn.softplus(step_raw[0] + dt_bias)
    log_rate = -jnp.exp(a_log) * step_size
    groups = local_len // GROUP
    x_heads = x_conv[0].reshape(groups, GROUP, heads_local, HEADDIM)
    b_rows = bc_conv[0, :, :STATE].reshape(groups, GROUP, STATE)
    c_rows = bc_conv[0, :, STATE:].reshape(groups, GROUP, STATE)
    step_groups = step_size.reshape(groups, GROUP, heads_local)
    log_decay = jnp.cumsum(log_rate.reshape(groups, GROUP, heads_local), axis=1)
    group_decay = jnp.exp(log_decay[:, -1, :])
    tail_weight = jnp.exp(log_decay[:, -1:, :] - log_decay) * step_groups
    weighted = (tail_weight[..., None] * x_heads.astype(jnp.float32)).astype(jnp.bfloat16)
    fresh_state = jnp.einsum("cshp,csn->chpn", weighted, b_rows, preferred_element_type=jnp.float32)

    def advance(carried_in, group_terms):
        state_now, decay_now = carried_in
        decay_group, fresh_group = group_terms
        return (
            (decay_group[:, None, None] * state_now + fresh_group, decay_now * decay_group),
            (state_now, decay_now),
        )

    zero_state = jnp.zeros((heads_local, HEADDIM, STATE), jnp.float32)
    (device_state, device_decay), (entry_local, entry_decay) = lax.scan(
        advance, (zero_state, jnp.ones((heads_local,), jnp.float32)), (group_decay, fresh_state)
    )
    intersection = jnp.einsum("ctn,csn->cts", c_rows, b_rows, preferred_element_type=jnp.float32)
    lower_mask = jnp.arange(GROUP)[:, None] >= jnp.arange(GROUP)[None, :]
    head_decay = jnp.swapaxes(log_decay, 1, 2)
    spread = head_decay[:, :, :, None] - head_decay[:, :, None, :]
    kernel = jnp.where(lower_mask, jnp.exp(jnp.where(lower_mask, spread, 0.0)), 0.0)
    mixing = (
        intersection[:, None] * kernel * jnp.swapaxes(step_groups, 1, 2)[:, :, None, :]
    ).astype(jnp.bfloat16)
    intra_out = jnp.einsum("chts,cshp->cthp", mixing, x_heads, preferred_element_type=jnp.float32)
    c_wide = c_rows.astype(jnp.float32)
    local_part = jnp.einsum("ctn,chpn->cthp", c_wide, entry_local, precision=lax.Precision.HIGHEST)
    incoming = entry_boundary(device_decay, device_state, zero_state)
    correction = jnp.einsum("ctn,hpn->cthp", c_wide, incoming, precision=lax.Precision.HIGHEST)
    carried = local_part + entry_decay[:, None, :, None] * correction
    outputs = intra_out + jnp.exp(log_decay)[..., None] * carried
    mixed_rows = outputs.reshape(local_len, heads_local, HEADDIM) + d_skip[None, :, None] * x_conv[
        0
    ].reshape(local_len, heads_local, HEADDIM).astype(jnp.float32)
    gated_rows = mixed_rows.reshape(local_len, feat_local) * jax.nn.silu(
        gate_in[0].astype(jnp.float32)
    )
    squares = lax.psum(jnp.sum(gated_rows * gated_rows, axis=1, keepdims=True), "head")
    mean_square = squares / DI
    result = (gated_rows * lax.rsqrt(mean_square + norm_eps) * norm_gain).astype(jnp.bfloat16)
    return result[None]


def solution(mesh):
    in_specs = (
        P(("member", "rep"), "seq", "head"),
        P(("member", "rep"), "seq", None),
        P(("member", "rep"), "seq", "head"),
        P(("member", "rep"), "seq", "head"),
        P("member", "head"),
        P(("member", "head")),
        P("member", None),
        P("member"),
        P(("member", "head")),
        P(("member", "head")),
        P(("member", "head")),
        P(("member", "head")),
    )
    out_specs = P(("member", "rep"), "seq", "head")
    return jax.shard_map(
        on_device, mesh=mesh, in_specs=in_specs, out_specs=out_specs, check_vma=False
    )
```

profile of v0, /device:TPU:24, one launch (start us, length us, event | category | flops | bytes accessed | tf_op | source)
XLA Modules:
  0.0 163.0 jit_solution(11498070673451994510)
XLA Ops:
  0.0 0.8 slice.71
  0.8 0.7 slice.72
  1.5 1.0 copy.43
  2.4 1.3 collective-permute-start.1
  3.7 1.1 reduce.5
  5.5 0.8 multiply_bitcast_fusion
  6.5 2.3 %reduce-window.6 = f32[4,20,2,128]{3,1,2,0:T(8,128)S(1)} reduce-window(f32[4,20,2,128]{3,1,2,0:T(8,128)S(1)} %copy.47, f32[]{:T(128)} %constant.26.clone.1), window={size=1x1x1x128 pad=0_0x0_0x0_0x127_0}, to_apply=%region_0.1 | reduce-window | flops 2600960 | bytes 163844 | tf_op jit(solution)/shard_map/reduce-window
  9.6 0.9 fusion.29
  10.4 0.9 convert_reduce_fusion.3
  11.4 0.8 slice_convert_fusion.3
  12.9 4.4 %copy.44 = bf16[1,1024,1280]{1,2,0:T(8,128)(2,1)} copy(bf16[1,1024,1280]{2,1,0:T(8,128)(2,1)} %param.16) | data formatting | bytes 5242880 | tf_op args[0]
  17.9 0.7 copy.58
  19.9 3.0 %copy.61 = bf16[1,1024,1280]{1,2,0:T(8,128)(2,1)S(1)} copy(bf16[1,1024,1280]{2,1,0:T(8,128)(2,1)} %param.18) | data formatting | bytes 5242880 | tf_op args[2]
  22.9 4.8 %reshape.188 = f32[4,256,20,64]{1,0,3,2:T(4,128)} reshape(bf16[1,1024,1280]{1,2,0:T(8,128)(2,1)S(1)} %copy.61) | data formatting | bytes 7864320 | tf_op jit(solution)/shard_map/convert_element_type | solution.py:119
  27.8 1.0 slice.93
  28.8 11.0 %multiply_convert_fusion.3 = bf16[1,1024,1280]{1,2,0:T(8,128)(2,1)S(1)} fusion(bf16[1,1024,1280]{1,2,0:T(8,128)(2,1)} %copy.44, bf16[1,3,1280]{1,2,0:T(8,128)(2,1)S(1)} %slice.93, f32[1280]{0:T(1024)S(1)} %get-tuple-element.98, f32[1280]{0:T(1024)S(1)} %get-tuple-element.99, f32[1280]{0:T(1024)S(1)} %get-tuple-element.97, f32[1280]{0:T(1024)S(1)} %get-tuple-element.96, ...), kind=kLoop, calls=%fused_computation.25 | loop fusion | flops 34078720 | bytes 5276160 | tf_op jit(solution)/shard_map/convert_element_type | solution.py:30
  39.9 3.8 %reshape_squeeze.10 = bf16[4,256,20,64]{1,0,3,2:T(4,128)(2,1)} reshape(bf16[1,1024,1280]{1,2,0:T(8,128)(2,1)S(1)} %multiply_convert_fusion.3) | data formatting | bytes 5242880 | tf_op jit(solution)/shard_map/reshape;squeeze | solution.py:78
  43.7 0.8 slice.98
  44.7 2.6 %multiply_convert_fusion.6 = bf16[1,1024,256]{2,1,0:T(8,128)(2,1)S(1)} fusion(bf16[1,1024,256]{2,1,0:T(8,128)(2,1)} %param.17, bf16[1,3,256]{2,1,0:T(4,128)(2,1)S(1)} %copy.46, f32[256]{0:T(256)S(1)} %bitcast.80, f32[256]{0:T(256)S(1)} %bitcast.81, f32[256]{0:T(256)S(1)} %bitcast.79, f32[256]{0:T(256)S(1)} %bitcast.78, f32[256]{0:T(256)S(1)} %convert_element_type.160), kind=kLoop, calls=%fused_computation.37 | loop fusion | flops 6815744 | bytes 1055232 | tf_op jit(solution)/shard_map/convert_element_type | solution.py:30
  47.3 4.2 %fusion.17 = f32[4,20,64,128]{3,2,1,0:T(8,128)} fusion(bf16[4,256,128,1]{2,1,3,0:T(8,128)(2,1)S(1)} %bitcast.72, f32[4,256,20]{1,2,0:T(8,128)} %copy.58, bf16[4,256,20,64]{1,0,3,2:T(4,128)(2,1)} %reshape_squeeze.10), kind=kOutput, calls=%fused_computation.32 | convolution fusion | flops 339476480 | bytes 5586944 | tf_op jit(solution)/shard_map/cshp,csn->chpn/dot_general | solution.py:86
  51.5 13.4 %while.28 = (s32[]{:T(128)}, f32[20,64,128]{2,1,0:T(8,128)S(1)}, f32[20]{0:T(128)S(1)}, f32[4,20,64,128]{3,2,1,0:T(8,128)}, f32[4,20]{1,0:T(4,128)}, /*index=5*/...) while((s32[]{:T(128)}, f32[20,64,128]{2,1,0:T(8,128)S(1)}, ...), condition=%wide.region_3.4_spmd.clone, body=%wide.region_2.3_spmd.clone.sunk | while | flops 655403 | bytes 3278069 | solution.py:97
  51.5 0.9 bitcast_dynamic-update-slice_fusion.2
  52.5 1.2 bitcast_add_fusion.3
  53.7 1.2 dynamic_update_slice.14
  54.9 0.9 bitcast_dynamic-update-slice_fusion.2
  55.9 1.2 bitcast_add_fusion.3
  57.1 1.2 dynamic_update_slice.14
  58.3 0.9 bitcast_dynamic-update-slice_fusion.2
  59.2 1.2 bitcast_add_fusion.3
  60.4 1.2 dynamic_update_slice.14
  61.6 0.9 bitcast_dynamic-update-slice_fusion.2
  62.5 1.2 bitcast_add_fusion.3
  63.7 1.2 dynamic_update_slice.14
  65.0 53.6 %while.27 = (s32[]{:T(128)}, f32[20,64,128]{2,1,0:T(8,128)S(1)}, f32[20]{0:T(128)S(1)}, f32[20,64,128]{2,1,0:T(8,128)S(1)}, s32[]{:T(128)}) while((s32[]{:T(128)}, f32[20,64,128]{2,1,0:T(8,128)S(1)}, f32[20]{0:T(128)S(1)}, f32[20,64,128]{2,1,0:T(8,128)S(1)}, s32[]{:T(128)}) %tuple.52), condition=%wide.region_5.6_spmd, body=%wide.region_4.5_spmd.sunk | while | flops 327682 | bytes 4587701 | solution.py:39
  65.1 1.3 collective-permute-start
  66.4 17.7 %collective-permute-done = f32[20,64,128]{2,1,0:T(8,128)S(1)} collective-permute-done((f32[20,64,128]{2,1,0:T(8,128)S(1)}, f32[20,64,128]{2,1,0:T(8,128)S(1)}, u32[]{:S(2)}, u32[]{:S(2)}) %collective-permute-start) | collective-permute-done | bytes 655392 | tf_op jit(solution)/shard_map/while/body/eval_jaxpr/ppermute | solution.py:19
  84.2 1.3 collective-permute-start
  85.5 16.2 %collective-permute-done = f32[20,64,128]{2,1,0:T(8,128)S(1)} collective-permute-done((f32[20,64,128]{2,1,0:T(8,128)S(1)}, f32[20,64,128]{2,1,0:T(8,128)S(1)}, u32[]{:S(2)}, u32[]{:S(2)}) %collective-permute-start) | collective-permute-done | bytes 655392 | tf_op jit(solution)/shard_map/while/body/eval_jaxpr/ppermute | solution.py:19
  101.9 1.3 collective-permute-start
  103.2 15.4 %collective-permute-done = f32[20,64,128]{2,1,0:T(8,128)S(1)} collective-permute-done((f32[20,64,128]{2,1,0:T(8,128)S(1)}, f32[20,64,128]{2,1,0:T(8,128)S(1)}, u32[]{:S(2)}, u32[]{:S(2)}) %collective-permute-start) | collective-permute-done | bytes 655392 | tf_op jit(solution)/shard_map/while/body/eval_jaxpr/ppermute | solution.py:19
  118.5 2.3 %fusion.22 = f32[4,256,20,64]{1,3,2,0:T(8,128)S(1)} fusion(bf16[4,256,128,1]{2,1,3,0:T(8,128)(2,1)S(1)} %bitcast.69, f32[20,64,128]{2,1,0:T(8,128)S(1)} %get-tuple-element.71), kind=kOutput, calls=%fused_computation.40 | convolution fusion | flops 2013265920 | bytes 6160384 | tf_op jit(solution)/shard_map/ctn,hpn->cthp/dot_general | solution.py:112
  120.9 2.2 %fusion.33 = f32[4,256,20,64]{1,3,2,0:T(8,128)S(1)} fusion(bf16[4,256,128,1]{2,1,3,0:T(8,128)(2,1)S(1)} %bitcast.70, f32[4,20,64,128]{3,2,1,0:T(8,128)S(1)} %copy-done.4), kind=kOutput, calls=%fused_computation.69 | convolution fusion | flops 2013265920 | bytes 8126464 | tf_op jit(solution)/shard_map/ctn,chpn->cthp/dot_general | solution.py:110
  124.3 9.7 %fusion.14 = (f32[4,256]{1,0:T(4,128)S(1)}, f32[4,256,20,64]{1,3,2,0:T(8,128)S(1)}) fusion(f32[4,256,20,64]{1,0,3,2:T(4,128)S(1)} %bitcast.68, f32[20]{0:T(128)S(1)} %copy-done.14, bf16[4,256,20,64]{1,0,3,2:T(4,128)(2,1)S(1)} %copy-done.3, f32[4,256,20,64]{1,3,2,0:T(8,128)S(1)} %fusion.33, f32[4,256,20,64]{1,3,2,0:T(8,128)S(1)} %fusion.22, ...), kind=kOutput, calls=%fused_computation.22 | convolution fusion | flops 720894976 | bytes 24957328 | tf_op jit(solution)/shard_map/chts,cshp->cthp/dot_general | solution.py:108
  134.0 6.2 %copy.60 = f32[4,256,20,64]{1,0,3,2:T(4,128)} copy(f32[4,256,20,64]{1,3,2,0:T(8,128)S(1)} %get-tuple-element.135) | data formatting | bytes 10485760 | tf_op jit(solution)/shard_map/add | solution.py:114
  140.2 7.9 %reshape.179 = f32[1,1024,1280]{1,2,0:T(8,128)} reshape(f32[4,256,20,64]{1,0,3,2:T(4,128)} %copy.60) | data formatting | bytes 10485760 | tf_op jit(solution)/shard_map/reshape | solution.py:115
  148.1 4.9 %psum.7 = f32[1024,1]{0,1:T(1,128)S(1)} all-reduce(f32[1024,1]{0,1:T(1,128)S(1)} %bitcast.77), channel_id=1, replica_groups=mesh['member'=2,'seq'=4,'head'=2,'rep'=2] {'head'}, use_global_device_ids=true, to_apply=%region_7.8 | all-reduce | flops 1024 | bytes 8192 | tf_op jit(solution)/shard_map/psum | solution.py:121
  153.1 5.5 %multiply_convert_fusion.2 = bf16[1,1024,1280]{1,2,0:T(8,128)(2,1)} fusion(f32[1,1024,1280]{1,2,0:T(8,128)} %reshape.179, bf16[1,1024,1280]{1,2,0:T(8,128)(2,1)S(1)} %copy-done.1, f32[1280]{0:T(1024)S(1)} %copy-done.11, f32[1024]{0:T(1024)S(1)} %bitcast.76, f32[1280]{0:T(1024)S(1)} %mul.235, bf16[1,1024,1280]{1,2,0:T(8,128)(2,1)} %copy-done.2), kind=kLoop, calls=%fused_computation.24 | loop fusion | flops 15728640 | bytes 13121536 | tf_op jit(solution)/shard_map/convert_element_type | solution.py:123
  158.6 4.4 %copy.64 = bf16[1,1024,1280]{2,1,0:T(8,128)(2,1)} copy(bf16[1,1024,1280]{1,2,0:T(8,128)(2,1)} %multiply_convert_fusion.2) | data formatting | bytes 5242880 | tf_op jit(solution)/shard_map/convert_element_type | solution.py:123
  (82 shorter events, 6.1 us)
Async XLA Ops:
  0.0 18.6 %copy-start.12 = (bf16[1280]{0:T(1024)(128)(2,1)S(1)}, bf16[1280]{0:T(1024)(128)(2,1)}, u32[]{:S(2)}) copy-start(bf16[1280]{0:T(1024)(128)(2,1)} %param.21) | copy-start | bytes 7684
  0.0 18.6 %copy-start.16 = (bf16[256]{0:T(256)(128)(2,1)S(1)}, bf16[256]{0:T(256)(128)(2,1)}, u32[]{:S(2)}) copy-start(bf16[256]{0:T(256)(128)(2,1)} %param.23) | copy-start | bytes 1540
  2.4 25.4 %collective-permute-start.1 = (bf16[1,3,1536]{1,2,0:T(8,128)(2,1)}, bf16[1,3,1536]{1,2,0:T(8,128)(2,1)}, u32[]{:S(2)}, u32[]{:S(2)}) collective-permute-start(bf16[1,3,1536]{1,2,0:T(8,128)(2,1)} %copy.43), channel_id=1, source_target_pairs={{0,4},{4,8},{8,12},{1,5},{5,9},{9,13},{2,6},{6,10},{10,14},{3,7},{... | collective-permute-start | bytes 27656 | tf_op jit(solution)/shard_map/ppermute | solution.py:19
  22.9 6.0 %copy-start.2 = (bf16[1,1024,1280]{1,2,0:T(8,128)(2,1)}, bf16[1,1024,1280]{1,2,0:T(8,128)(2,1)S(1)}, u32[]{:S(2)}) copy-start(bf16[1,1024,1280]{1,2,0:T(8,128)(2,1)S(1)} %copy.61) | copy-start | bytes 7864324
  22.9 4.8 %copy-start.13 = (f32[20]{0:T(128)S(1)}, f32[20]{0:T(128)}, u32[]{:S(2)}) copy-start(f32[20]{0:T(128)} %param.26) | copy-start | bytes 244
  39.9 11.7 %copy-start = (bf16[1,1024,1280]{1,2,0:T(8,128)(2,1)}, bf16[1,1024,1280]{1,2,0:T(8,128)(2,1)S(1)}, u32[]{:S(2)}) copy-start(bf16[1,1024,1280]{1,2,0:T(8,128)(2,1)S(1)} %multiply_convert_fusion.3) | copy-start | bytes 7864324
  47.3 4.3 %copy-start.5 = (bf16[1,1024,128]{2,1,0:T(8,128)(2,1)}, bf16[1,1024,128]{2,1,0:T(8,128)(2,1)S(1)}, u32[]{:S(2)}) copy-start(bf16[1,1024,128]{2,1,0:T(8,128)(2,1)S(1)} %get-tuple-element.125) | copy-start | bytes 786436
  65.1 19.0 %collective-permute-start = (f32[20,64,128]{2,1,0:T(8,128)S(1)}, f32[20,64,128]{2,1,0:T(8,128)S(1)}, u32[]{:S(2)}, u32[]{:S(2)}) collective-permute-start(f32[20,64,128]{2,1,0:T(8,128)S(1)} %multiply_add_fusion.2), channel_id=1, source_target_pairs={{0,4},{4,8},{8,12},{1,5},{5,9},{9,13},{2,6},{6,10},{10,14},{3,7},{... | collective-permute-start | bytes 1966088 | tf_op jit(solution)/shard_map/while/body/eval_jaxpr/ppermute | solution.py:19
  84.2 17.5 %collective-permute-start = (f32[20,64,128]{2,1,0:T(8,128)S(1)}, f32[20,64,128]{2,1,0:T(8,128)S(1)}, u32[]{:S(2)}, u32[]{:S(2)}) collective-permute-start(f32[20,64,128]{2,1,0:T(8,128)S(1)} %multiply_add_fusion.2), channel_id=1, source_target_pairs={{0,4},{4,8},{8,12},{1,5},{5,9},{9,13},{2,6},{6,10},{10,14},{3,7},{... | collective-permute-start | bytes 1966088 | tf_op jit(solution)/shard_map/while/body/eval_jaxpr/ppermute | solution.py:19
  101.9 16.7 %collective-permute-start = (f32[20,64,128]{2,1,0:T(8,128)S(1)}, f32[20,64,128]{2,1,0:T(8,128)S(1)}, u32[]{:S(2)}, u32[]{:S(2)}) collective-permute-start(f32[20,64,128]{2,1,0:T(8,128)S(1)} %multiply_add_fusion.2), channel_id=1, source_target_pairs={{0,4},{4,8},{8,12},{1,5},{5,9},{9,13},{2,6},{6,10},{10,14},{3,7},{... | collective-permute-start | bytes 1966088 | tf_op jit(solution)/shard_map/while/body/eval_jaxpr/ppermute | solution.py:19
  118.5 2.4 %copy-start.4 = (f32[4,20,64,128]{3,2,1,0:T(8,128)S(1)}, f32[4,20,64,128]{3,2,1,0:T(8,128)}, u32[]{:S(2)}) copy-start(f32[4,20,64,128]{3,2,1,0:T(8,128)} %get-tuple-element.67) | copy-start | bytes 7864324
  120.8 2.3 %copy-start.6 = (bf16[1,1024,128]{2,1,0:T(8,128)(2,1)S(1)}, bf16[1,1024,128]{2,1,0:T(8,128)(2,1)}, u32[]{:S(2)}) copy-start(bf16[1,1024,128]{2,1,0:T(8,128)(2,1)} %copy-done.5) | copy-start | bytes 786436
  120.8 2.6 %slice-start = ((s8[5242880]{0:T(1024)(128)(4,1)}), s8[4194304]{0:T(1024)(128)(4,1)S(1)}, s32[]{:S(2)}) async-start(s8[5242880]{0:T(1024)(128)(4,1)} %bitcast.67), calls=%async_computation | async-start | bytes 8388608
  120.8 3.1 %copy-start.3 = (bf16[4,256,20,64]{1,0,3,2:T(4,128)(2,1)S(1)}, bf16[4,256,20,64]{1,0,3,2:T(4,128)(2,1)}, u32[]{:S(2)}) copy-start(bf16[4,256,20,64]{1,0,3,2:T(4,128)(2,1)} %reshape_squeeze.10) | copy-start | bytes 7864324
  120.8 3.1 %copy-start.7 = (f32[4,20,256]{2,1,0:T(8,128)S(1)}, f32[4,20,256]{2,1,0:T(8,128)}, u32[]{:S(2)}) copy-start(f32[4,20,256]{2,1,0:T(8,128)} %copy.51) | copy-start | bytes 245764
  120.9 3.1 %copy-start.8 = (f32[4,20,256]{2,1,0:T(8,128)S(1)}, f32[4,20,256]{2,1,0:T(8,128)}, u32[]{:S(2)}) copy-start(f32[4,20,256]{2,1,0:T(8,128)} %copy.53) | copy-start | bytes 245764
  120.9 3.1 %copy-start.9 = (f32[4,256,20]{1,2,0:T(8,128)S(1)}, f32[4,256,20]{1,2,0:T(8,128)}, u32[]{:S(2)}) copy-start(f32[4,256,20]{1,2,0:T(8,128)} %copy.55) | copy-start | bytes 245764
  120.9 3.0 %copy-start.10 = (pred[256,256]{1,0:T(8,128)(4,1)S(1)}, pred[256,256]{1,0:T(8,128)(4,1)}, u32[]{:S(2)}) copy-start(pred[256,256]{1,0:T(8,128)(4,1)} %iota_compare_fusion) | copy-start | bytes 196612
  120.9 3.0 %copy-start.14 = (f32[20]{0:T(128)S(1)}, f32[20]{0:T(128)}, u32[]{:S(2)}) copy-start(f32[20]{0:T(128)} %param.26) | copy-start | bytes 244
  120.9 3.0 %copy-start.15 = (f32[4,20]{1,0:T(4,128)S(1)}, f32[4,20]{1,0:T(4,128)}, u32[]{:S(2)}) copy-start(f32[4,20]{1,0:T(4,128)} %get-tuple-element.68) | copy-start | bytes 964
  120.9 3.3 %slice-start.1 = ((s8[5242880]{0:T(1024)(128)(4,1)}), s8[1048576]{0:T(1024)(128)(4,1)S(1)}, s32[]{:S(2)}) async-start(s8[5242880]{0:T(1024)(128)(4,1)} %bitcast.67), calls=%async_computation.1 | async-start | bytes 2097152
  140.2 12.8 %copy-start.1 = (bf16[1,1024,1280]{1,2,0:T(8,128)(2,1)S(1)}, bf16[1,1024,1280]{1,2,0:T(8,128)(2,1)}, u32[]{:S(2)}) copy-start(bf16[1,1024,1280]{1,2,0:T(8,128)(2,1)} %copy-done) | copy-start | bytes 7864324
  140.2 12.8 %copy-start.11 = (f32[1280]{0:T(1024)S(1)}, f32[1280]{0:T(1024)}, u32[]{:S(2)}) copy-start(f32[1280]{0:T(1024)} %param.27) | copy-start | bytes 15364
where the time goes:
time: 165 us; the launch traced here: 163 us
  waiting for transfers between devices  49.3 us (30%)
  local copies, waits for them, and re-layouts  48 us (29%)
  other arithmetic  36.4 us (22%)
  matrix products  18.8 us (11%)
  starting transfers between devices  5.16 us (3%)
  blocking collectives  4.92 us (3%)
    ppermute x4, waiting for transfers between devices, passed_along(): return lax.ppermute(value, axis, pairs)  49.3 us
    convert_element_type x2, other arithmetic, shard_conv(): return jax.nn.silu(summed).astype(jnp.bfloat16)  13.6 us
    dot_general x1, matrix products, on_device(): jnp.einsum('chts,cshp->cthp', mixing, x_heads, preferred_element_type=jnp...  9.74 us
    unnamed x41, local copies, waits for them, and re-layouts  8.23 us
    reshape x1, local copies, waits for them, and re-layouts, on_device(): outputs.reshape(local_len, heads_local, HEADDIM)  7.85 us
    add x1, local copies, waits for them, and re-layouts, on_device(): outputs = intra_out + jnp.exp(log_decay)[..., None] * carried  6.22 us
    convert_element_type x1, other arithmetic, on_device(): (gated_rows * lax.rsqrt(mean_square + norm_eps) * norm_gain).astype(jnp.b...  5.55 us
    ppermute x4, starting transfers between devices, passed_along(): return lax.ppermute(value, axis, pairs)  5.16 us
  transfers between devices with their start and end apart: 4, of which 3 were waited for; matrix products, arithmetic and copies ran while one was open for 15% of the time, Pallas kernels for 0%

commit v1 on v0

v1 whole, which is shorter than its diff:
```python
import functools

import jax
import jax.numpy as jnp
from jax import lax
from jax.experimental import pallas as pl
from jax.experimental.pallas import tpu as pltpu
from jax.sharding import PartitionSpec as P

HEADDIM = 64
STATE = 128
GROUP = 256
CONV = 4
LANE = 128
HALO = 16

norm_eps = 1e-05
F32 = jnp.float32
BF16 = jnp.bfloat16
MESH = pl.DeviceIdType.MESH


def silu(v):
    half = 0.5 * v
    return half * jnp.tanh(half) + half


def pad_lanes(v):
    rows, cols = v.shape
    return jnp.concatenate((v, jnp.zeros((rows, LANE - cols), v.dtype)), axis=1)


def split_pair(v):
    hi = v.astype(BF16).astype(F32)
    lo = v - hi
    lane = lax.broadcasted_iota(jnp.int32, v.shape, 1)
    return jnp.where(lane < 64, hi, pltpu.roll(lo, 64, 1)).astype(BF16)


def mm(a, b):
    return jnp.dot(a, b, preferred_element_type=F32)


def kernel(
    n_seq,
    n_head,
    x_hbm,
    bc_hbm,
    gate_hbm,
    step_hbm,
    wx_ref,
    bx_ref,
    wbc_ref,
    bbc_ref,
    dt_ref,
    alog_ref,
    dskip_ref,
    gain_ref,
    out_hbm,
    xin,
    bcin,
    gate,
    stepin,
    xc,
    bcc,
    bt,
    ld,
    step,
    ldt,
    stept,
    expand,
    wtd,
    fresh,
    gd,
    state,
    state2,
    decay,
    dsk,
    inter,
    y,
    outv,
    tx,
    rx,
    ss_tx,
    ss_rx,
    in_sem,
    out_sem,
    halo_send,
    halo_recv,
    tx_sem,
    rx_sem,
    ss_send,
    ss_recv,
):
    length, feat = xc.shape
    heads = feat // HEADDIM
    groups = length // GROUP
    tiles = feat // LANE
    n_chunk, _, chunk_w = tx.shape
    di = feat * n_head
    me = lax.axis_index("seq")
    me_head = lax.axis_index("head")
    first = me == 0
    last = me == n_seq - 1

    def rows(b):
        return pl.ds(pl.multiple_of(b * GROUP, GROUP), GROUP)

    def rows_in(b):
        return pl.ds(pl.multiple_of(b * GROUP + HALO, HALO), GROUP)

    step_copy = pltpu.make_async_copy(step_hbm.at[0], stepin, in_sem.at[0])
    bc_copy = pltpu.make_async_copy(bc_hbm.at[0], bcin.at[pl.ds(HALO, length)], in_sem.at[1])

    def x_copy(b):
        return pltpu.make_async_copy(x_hbm.at[0, rows(b)], xin.at[rows_in(b)], in_sem.at[2 + b])

    gate_copy = pltpu.make_async_copy(gate_hbm.at[0], gate, in_sem.at[2 + groups])
    step_copy.start()
    bc_copy.start()
    for b in range(groups):
        x_copy(b).start()
    gate_copy.start()

    barrier = pltpu.get_barrier_semaphore()

    @pl.when(jnp.logical_not(first))
    def _():
        pl.semaphore_signal(barrier, inc=1, device_id={"seq": me - 1}, device_id_type=MESH)

    @pl.when(jnp.logical_not(last))
    def _():
        pl.semaphore_signal(barrier, inc=1, device_id={"seq": me + 1}, device_id_type=MESH)

    def mate(r):
        return lax.rem(me_head + r, n_head)

    for r in range(1, n_head):
        pl.semaphore_signal(barrier, inc=1, device_id={"head": mate(r)}, device_id_type=MESH)

    k_of = lax.rem(lax.broadcasted_iota(jnp.int32, (LANE, feat), 0), 64)
    h_of = lax.broadcasted_iota(jnp.int32, (LANE, feat), 1) // HEADDIM
    expand[...] = jnp.where(k_of == h_of, 1.0, 0.0).astype(BF16)
    dsk[...] = mm(
        split_pair(jnp.broadcast_to(pad_lanes(dskip_ref[...]), (8, LANE))), expand[...]
    )

    peers = n_head - 1 + jnp.where(first, 0, 1) + jnp.where(last, 0, 1)
    pl.semaphore_wait(barrier, peers)

    halo_x = pltpu.make_async_remote_copy(
        src_ref=x_hbm.at[0, pl.ds(length - HALO, HALO)],
        dst_ref=xin.at[pl.ds(0, HALO)],
        send_sem=halo_send.at[0],
        recv_sem=halo_recv.at[0],
        device_id={"seq": me + 1},
        device_id_type=MESH,
    )
    halo_bc = pltpu.make_async_remote_copy(
        src_ref=bc_hbm.at[0, pl.ds(length - HALO, HALO)],
        dst_ref=bcin.at[pl.ds(0, HALO)],
        send_sem=halo_send.at[1],
        recv_sem=halo_recv.at[1],
        device_id={"seq": me + 1},
        device_id_type=MESH,
    )

    @pl.when(jnp.logical_not(last))
    def _():
        halo_x.start()
        halo_bc.start()

    @pl.when(first)
    def _():
        xin[0:HALO, :] = jnp.zeros((HALO, feat), BF16)
        bcin[0:HALO, :] = jnp.zeros((HALO, 2 * STATE), BF16)
        rx[...] = jnp.zeros(rx.shape, BF16)

    step_copy.wait()
    dt_row = dt_ref[...]
    rate_row = -jnp.exp(alog_ref[...])
    tri = (
        lax.broadcasted_iota(jnp.int32, (GROUP, GROUP), 0)
        >= lax.broadcasted_iota(jnp.int32, (GROUP, GROUP), 1)
    )
    tri_ones = jnp.where(tri, 1.0, 0.0).astype(BF16)

    def decay_body(b, carry):
        v = stepin[rows(b), :] + dt_row
        size = jnp.maximum(v, 0.0) + jnp.log1p(jnp.exp(-jnp.abs(v)))
        rate = pad_lanes(rate_row * size)
        size = pad_lanes(size)
        hi = rate.astype(BF16)
        rest = rate - hi.astype(F32)
        mid = rest.astype(BF16)
        low = (rest - mid.astype(F32)).astype(BF16)
        total = mm(tri_ones, hi) + mm(tri_ones, mid) + mm(tri_ones, low)
        ld[rows(b), :] = total
        step[rows(b), :] = size
        ldt[b] = total.T[0 : ldt.shape[1]]
        stept[b] = size.T[0 : ldt.shape[1]]
        return carry

    lax.fori_loop(0, groups, decay_body, 0)
    bc_copy.wait()

    def conv(src, start, lo, weight, bias):
        ext = src[pl.ds(pl.multiple_of(start, HALO), GROUP + HALO), lo : lo + LANE].astype(F32)
        w = weight[:, lo : lo + LANE].astype(F32)
        total = bias[0:1, lo : lo + LANE].astype(F32)
        for k in range(CONV):
            off = HALO - CONV + 1 + k
            total = total + w[k : k + 1] * ext[off : off + GROUP]
        return silu(total)

    def fresh_body(i, carry):
        b = lax.rem(i + 1, groups)

        @pl.when(b > 0)
        def _():
            x_copy(b).wait()

        @pl.when(jnp.logical_and(b == 0, jnp.logical_not(first)))
        def _():
            halo_x.wait_recv()
            halo_bc.wait_recv()

        start = b * GROUP
        b_part = conv(bcin, start, 0, wbc_ref, bbc_ref).astype(BF16)
        bcc[rows(b), 0:STATE] = b_part
        bcc[rows(b), STATE : 2 * STATE] = conv(bcin, start, STATE, wbc_ref, bbc_ref).astype(BF16)
        bt[b] = b_part.astype(F32).T.astype(BF16)
        ld_b = ld[rows(b), :]
        end = ld_b[GROUP - 1 : GROUP]
        tail = split_pair(jnp.exp(end - ld_b) * step[rows(b), :])
        gd[b] = mm(split_pair(jnp.broadcast_to(jnp.exp(end), (8, LANE))), expand[...])
        for j in range(tiles):
            lo = j * LANE
            v = conv(xin, start, lo, wx_ref, bx_ref).astype(BF16)
            xc[rows(b), lo : lo + LANE] = v
            weight = mm(tail, expand[:, lo : lo + LANE])
            wtd[:, lo : lo + LANE] = (weight * v.astype(F32)).astype(BF16)
        fresh[b] = mm(bt[b], wtd[...])
        return carry

    x_copy(0).wait()
    lax.fori_loop(0, groups, fresh_body, 0)

    total_state = fresh[0]
    total_decay = gd[0]
    for b in range(1, groups):
        total_state = gd[b, 0:1] * total_state + fresh[b]
        total_decay = total_decay * gd[b]
    state[...] = total_state
    decay[...] = total_decay

    def relay_copy(c):
        return pltpu.make_async_remote_copy(
            src_ref=tx.at[c],
            dst_ref=rx.at[c],
            send_sem=tx_sem.at[c],
            recv_sem=rx_sem.at[c],
            device_id={"seq": me + 1},
            device_id_type=MESH,
        )

    @pl.when(jnp.logical_and(first, jnp.logical_not(last)))
    def _():
        for c in range(n_chunk):
            tx[c] = state[:, c * chunk_w : (c + 1) * chunk_w].astype(BF16)
            relay_copy(c).start()

    def relay(c):
        relay_copy(c).wait_recv()

        @pl.when(jnp.logical_not(last))
        def _():
            cols = pl.ds(pl.multiple_of(c * chunk_w, LANE), chunk_w)
            tx[c] = (decay[0:1, cols] * rx[c].astype(F32) + state[:, cols]).astype(BF16)
            relay_copy(c).start()

    half = GROUP // 2
    low_mask = jnp.where(
        lax.broadcasted_iota(jnp.int32, (1, LANE), 1) < HEADDIM, 1.0, 0.0
    ).astype(BF16)
    high_mask = (1.0 - low_mask.astype(F32)).astype(BF16)
    lag = jnp.minimum(me, 3)
    points = max(1, -(-(n_chunk + 3) // groups))
    marks = [(q + 1) * tiles // points - 1 for q in range(points)]

    def intra_body(b, carry):
        inter[...] = mm(bcc[rows(b), STATE : 2 * STATE], bt[b])
        tri_half = (
            lax.broadcasted_iota(jnp.int32, (half, half), 0)
            >= lax.broadcasted_iota(jnp.int32, (half, half), 1)
        )
        for j in range(tiles):
            lo = j * LANE
            x_pair = xc[rows(b), lo : lo + LANE]
            parts = []
            for e in range(2):
                h = 2 * j + e
                x_own = x_pair * (low_mask if e == 0 else high_mask)
                col = ld[rows(b), h : h + 1]
                row = ldt[b, h : h + 1, :]
                size = stept[b, h : h + 1, :]
                quad = {}
                for ti, si in ((0, 0), (1, 0), (1, 1)):
                    ts, sl = slice(ti * half, (ti + 1) * half), slice(si * half, (si + 1) * half)
                    m = inter[ts, sl] * jnp.exp(col[ts] - row[:, sl]) * size[:, sl]
                    if ti == si:
                        m = jnp.where(tri_half, m, 0.0)
                    quad[ti, si] = m.astype(BF16)
                top = mm(quad[0, 0], x_own[:half])
                bottom = mm(jnp.concatenate((quad[1, 0], quad[1, 1]), axis=1), x_own)
                parts.append((top, bottom))
            skip = dsk[0:1, lo : lo + LANE]
            for ti in range(2):
                at = pl.ds(pl.multiple_of(b * GROUP + ti * half, half), half)
                y[at, lo : lo + LANE] = (
                    parts[0][ti]
                    + parts[1][ti]
                    + skip * x_pair[ti * half : (ti + 1) * half].astype(F32)
                )
            if j in marks:
                c = b * points + marks.index(j) - lag

                @pl.when(
                    jnp.logical_and(
                        jnp.logical_not(first), jnp.logical_and(c >= 0, c < n_chunk)
                    )
                )
                def _():
                    relay(c)

        return carry

    lax.fori_loop(0, groups, intra_body, 0)
    gate_copy.wait()

    for c in range(n_chunk):
        state[:, c * chunk_w : (c + 1) * chunk_w] = rx[c].astype(F32)

    def ss_copy(b, r):
        return pltpu.make_async_remote_copy(
            src_ref=ss_tx.at[b],
            dst_ref=ss_rx.at[b, r],
            send_sem=ss_send.at[b, r],
            recv_sem=ss_recv.at[b, r],
            device_id={"head": mate(r)},
            device_id_type=MESH,
        )

    def gate_body(b, carry):
        now = state[...]
        hi = now.astype(BF16)
        state2[0:STATE, :] = hi
        state2[STATE : 2 * STATE, :] = (now - hi.astype(F32)).astype(BF16)
        state[...] = gd[b, 0:1] * now + fresh[b]
        c_part = bcc[rows(b), STATE : 2 * STATE]
        c_twice = jnp.concatenate((c_part, c_part), axis=1)
        entry = split_pair(jnp.exp(ld[rows(b), :]))
        acc = jnp.zeros((GROUP, LANE), F32)
        for j in range(tiles):
            cols = slice(j * LANE, (j + 1) * LANE)
            carried = mm(c_twice, state2[:, cols])
            scale = mm(entry, expand[:, cols])
            z = (y[rows(b), cols] + scale * carried) * silu(gate[rows(b), cols].astype(F32))
            y[rows(b), cols] = z
            acc = acc + z * z
        sums = jnp.sum(acc.T, axis=0, keepdims=True)
        ss_tx[b] = jnp.broadcast_to(sums, (8, GROUP))
        for r in range(1, n_head):
            ss_copy(b, r).start()
        return carry

    lax.fori_loop(0, groups, gate_body, 0)

    def out_copy(b):
        return pltpu.make_async_copy(outv.at[rows(b)], out_hbm.at[0, rows(b)], out_sem.at[b])

    def norm_body(b, carry):
        sums = ss_tx[b, 0:1]
        for r in range(1, n_head):
            ss_copy(b, r).wait_recv()
            sums = sums + ss_rx[b, r, 0:1]
        scale = lax.rsqrt(sums * (1.0 / di) + norm_eps)
        scale = jnp.broadcast_to(scale, (LANE, GROUP)).T
        for j in range(tiles):
            cols = slice(j * LANE, (j + 1) * LANE)
            outv[rows(b), cols] = (y[rows(b), cols] * scale * gain_ref[0:1, cols]).astype(BF16)
        out_copy(b).start()
        return carry

    lax.fori_loop(0, groups, norm_body, 0)

    for b in range(groups):
        out_copy(b).wait()
        for r in range(1, n_head):
            ss_copy(b, r).wait_send()

    @pl.when(jnp.logical_not(last))
    def _():
        halo_x.wait_send()
        halo_bc.wait_send()
        for c in range(n_chunk):
            relay_copy(c).wait_send()


def on_device(
    x_raw,
    bc_raw,
    gate_in,
    step_raw,
    conv_x_weight,
    conv_x_bias,
    conv_bc_weight,
    conv_bc_bias,
    dt_bias,
    a_log,
    d_skip,
    norm_gain,
):
    length, feat = x_raw.shape[1], x_raw.shape[2]
    heads = dt_bias.shape[0]
    groups = length // GROUP
    tiles = feat // LANE
    n_seq, n_head = lax.axis_size("seq"), lax.axis_size("head")
    n_chunk = tiles // 2 if tiles % 2 == 0 else tiles
    chunk_w = feat // n_chunk
    head_rows = -(-heads // 8) * 8
    anyspec = pl.BlockSpec(memory_space=pl.ANY)
    vspec = pl.BlockSpec(memory_space=pltpu.VMEM)
    V = pltpu.VMEM
    DMA = pltpu.SemaphoreType.DMA
    call = pl.pallas_call(
        functools.partial(kernel, n_seq, n_head),
        out_shape=jax.ShapeDtypeStruct(x_raw.shape, BF16),
        in_specs=[anyspec] * 4 + [vspec] * 8,
        out_specs=anyspec,
        scratch_shapes=[
            V((HALO + length, feat), BF16),
            V((HALO + length, 2 * STATE), BF16),
            V((length, feat), BF16),
            V((length, heads), F32),
            V((length, feat), BF16),
            V((length, 2 * STATE), BF16),
            V((groups, STATE, GROUP), BF16),
            V((length, LANE), F32),
            V((length, LANE), F32),
            V((groups, head_rows, GROUP), F32),
            V((groups, head_rows, GROUP), F32),
            V((LANE, feat), BF16),
            V((GROUP, feat), BF16),
            V((groups, STATE, feat), F32),
            V((groups, 8, feat), F32),
            V((STATE, feat), F32),
            V((2 * STATE, feat), BF16),
            V((8, feat), F32),
            V((8, feat), F32),
            V((GROUP, GROUP), F32),
            V((length, feat), F32),
            V((length, feat), BF16),
            V((n_chunk, STATE, chunk_w), BF16),
            V((n_chunk, STATE, chunk_w), BF16),
            V((groups, 8, GROUP), F32),
            V((groups, n_head, 8, GROUP), F32),
            DMA((3 + groups,)),
            DMA((groups,)),
            DMA((2,)),
            DMA((2,)),
            DMA((n_chunk,)),
            DMA((n_chunk,)),
            DMA((groups, n_head)),
            DMA((groups, n_head)),
        ],
        compiler_params=pltpu.CompilerParams(collective_id=0, has_side_effects=True),
        name="ssd_layer",
    )
    return call(
        x_raw,
        bc_raw,
        gate_in,
        step_raw,
        conv_x_weight,
        conv_x_bias[None],
        conv_bc_weight,
        conv_bc_bias[None],
        dt_bias[None],
        a_log[None],
        d_skip[None],
        norm_gain[None],
    )


def solution(mesh):
    in_specs = (
        P(("member", "rep"), "seq", "head"),
        P(("member", "rep"), "seq", None),
        P(("member", "rep"), "seq", "head"),
        P(("member", "rep"), "seq", "head"),
        P("member", "head"),
        P(("member", "head")),
        P("member", None),
        P("member"),
        P(("member", "head")),
        P(("member", "head")),
        P(("member", "head")),
        P(("member", "head")),
    )
    out_specs = P(("member", "rep"), "seq", "head")
    return jax.shard_map(
        on_device, mesh=mesh, in_specs=in_specs, out_specs=out_specs, check_vma=False
    )
```

time: 165 us -> 44.8 us (0.27); the launches traced: 163 us -> 44.5 us
  waiting for transfers between devices: 49.3 us -> 0 us
  local copies, waits for them, and re-layouts: 48 us -> 9.12 us
  other arithmetic: 36.4 us -> 0 us
  Pallas kernels: 0 us -> 35.4 us
  matrix products: 18.8 us -> 0 us
  starting transfers between devices: 5.16 us -> 0 us
  blocking collectives: 4.92 us -> 0 us
    ppermute x4 -> x0, waiting for transfers between devices: 49.3 us -> none  [passed_along(): return lax.ppermute(value, axis, pairs)]
    pallas_call x0 -> x1, Pallas kernels: none -> 35.4 us  [on_device(): call(x_raw, bc_raw, gate_in, step_raw, conv_x_weight, conv_x_bias[None],...]
    convert_element_type x7 -> x0, other arithmetic: 20.9 us -> none  [the longest x2 13.6 us: shard_conv(): return jax.nn.silu(summed).astype(jnp.bfloat16)]
    dot_general x5 -> x0, matrix products: 18.8 us -> none  [the longest x1 9.74 us: on_device(): jnp.einsum('chts,cshp->cthp', mixing, x_heads, preferred_element_type=jnp...]
    convert_element_type x2 -> x0, local copies, waits for them, and re-layouts: 9.16 us -> none  [the longest x1 4.78 us: on_device(): gate_in[0].astype(jnp.float32)]
    reshape x3 -> x0, local copies, waits for them, and re-layouts: 7.93 us -> none  [the longest x1 7.85 us: on_device(): outputs.reshape(local_len, heads_local, HEADDIM)]
    add x1 -> x0, local copies, waits for them, and re-layouts: 6.22 us -> none  [on_device(): outputs = intra_out + jnp.exp(log_decay)[..., None] * carried]
    add x7 -> x0, other arithmetic: 5.24 us -> none  [the longest x4 4.87 us: advance(): decay_group[:, None, None] * state_now + fresh_group]
  transfers between devices with their start and end apart: 4 -> 0, of which waited for: 3 -> 0; matrix products, arithmetic and copies ran while one was open for 15% -> 0% of each run, Pallas kernels for 0% -> 0%
where the time goes in v1:
time: 44.8 us; the launch traced here: 44.5 us
  Pallas kernels  35.4 us (79%)
  local copies, waits for them, and re-layouts  9.12 us (20%)
    pallas_call x1, Pallas kernels, on_device(): call(x_raw, bc_raw, gate_in, step_raw, conv_x_weight, conv_x_bias[None],...  35.4 us
    unnamed x2, local copies, waits for them, and re-layouts  5.3 us
    broadcast_in_dim x1, local copies, waits for them, and re-layouts, on_device(): norm_gain[None]  1.29 us
    broadcast_in_dim x1, local copies, waits for them, and re-layouts, on_device(): conv_x_bias[None]  1.28 us
    broadcast_in_dim x1, local copies, waits for them, and re-layouts, on_device(): conv_bc_bias[None]  1.25 us

profile of v1, /device:TPU:24, one launch (start us, length us, event | category | flops | bytes accessed | tf_op | source)
XLA Modules:
  0.0 44.5 jit_solution(6259043274549271683)
XLA Ops:
  0.0 1.2 %broadcast_in_dim.19.bbc_ref = bf16[1,256]{1,0:T(2,128)(2,1)} reshape(bf16[256]{0:T(256)(128)(2,1)} %param.19) | data formatting | bytes 1024 | tf_op jit(solution)/shard_map/broadcast_in_dim | solution.py:488
  1.2 1.3 %broadcast_in_dim.18.bx_ref = bf16[1,1280]{1,0:T(2,128)(2,1)} reshape(bf16[1280]{0:T(1024)(128)(2,1)} %param.17) | data formatting | bytes 5120 | tf_op jit(solution)/shard_map/broadcast_in_dim | solution.py:486
  2.5 1.3 %broadcast_in_dim.23.gain_ref = f32[1,1280]{1,0:T(1,128)} reshape(f32[1280]{0:T(1024)} %param.23) | data formatting | bytes 10240 | tf_op jit(solution)/shard_map/broadcast_in_dim | solution.py:492
  3.8 1.9 %copy.13.step_hbm = f32[1,1024,20]{2,1,0:T(8,128)} copy(f32[1,1024,20]{1,0,2:T(1,128)} %param.15) | data formatting | bytes 163840 | tf_op args[3]
  5.7 35.4 %ssd_layer.1 = bf16[1,1024,1280]{2,1,0:T(8,128)(2,1)} custom-call(bf16[1,1024,1280]{2,1,0:T(8,128)(2,1)} %x_hbm.1, bf16[1,1024,256]{2,1,0:T(8,128)(2,1)} %bc_hbm.1, bf16[1,1024,1280]{2,1,0:T(8,128)(2,1)} %gate_hbm.1, f32[1,1024,20]{2,1,0:T(8,128)} %copy.13.step_hbm, bf16[4,1280]{1,0:T(4,128)(2,1)} %wx_ref.1, bf16[1,1280]{1,0:T(2,128)(2,1)} %broadcast_in_dim.18.bx_ref, ...), custom_call_target="tpu_custom_call" | custom-call | tf_op jit(solution)/shard_map/ssd_layer/pallas_call | solution.py:480
  41.1 3.4 %copy.15 = bf16[1,1024,1280]{2,1,0:T(8,128)(2,1)} copy(bf16[1,1024,1280]{2,1,0:T(8,128)(2,1)} %ssd_layer.1) | data formatting | bytes 5242880

commit v2 on v1

v2 whole, which is shorter than its diff:
```python
import functools

import jax
import jax.numpy as jnp
from jax import lax
from jax.experimental import pallas as pl
from jax.experimental.pallas import tpu as pltpu
from jax.sharding import PartitionSpec as P

HEADDIM = 64
STATE = 128
GROUP = 256
CONV = 4
LANE = 128
HALO = 16
LOG2E = 1.4426950408889634

norm_eps = 1e-05
F32 = jnp.float32
BF16 = jnp.bfloat16
MESH = pl.DeviceIdType.MESH


def silu(v):
    half = 0.5 * v
    return half * jnp.tanh(half) + half


def pad_lanes(v):
    rows, cols = v.shape
    return jnp.concatenate((v, jnp.zeros((rows, LANE - cols), v.dtype)), axis=1)


def split_pair(v):
    hi = v.astype(BF16).astype(F32)
    lo = v - hi
    lane = lax.broadcasted_iota(jnp.int32, v.shape, 1)
    return jnp.where(lane < 64, hi, pltpu.roll(lo, 64, 1)).astype(BF16)


def to_column(row):
    return jnp.broadcast_to(pad_lanes(row), (LANE, LANE)).T[:, 0:1]


def mm(a, b):
    return jnp.dot(a, b, preferred_element_type=F32)


def kernel(
    n_seq,
    n_head,
    x_hbm,
    bc_hbm,
    gate_hbm,
    step_hbm,
    wx_ref,
    bx_ref,
    wbc_ref,
    bbc_ref,
    dt_ref,
    alog_ref,
    dskip_ref,
    y,
    sums_out,
    xin,
    bcin,
    gate,
    stepin,
    xc,
    bcc,
    bt,
    ld,
    step,
    ldt,
    stept,
    ext,
    xtap,
    btap,
    tail,
    acc,
    expand,
    wtd,
    fresh,
    gd,
    state,
    decay,
    dsk,
    inter,
    tx,
    rx,
    ss_tx,
    ss_rx,
    in_sem,
    halo_send,
    halo_recv,
    tx_sem,
    rx_sem,
    ss_send,
    ss_recv,
):
    length, feat = xc.shape
    heads = feat // HEADDIM
    groups = length // GROUP
    tiles = feat // LANE
    n_chunk, _, chunk_w = tx.shape
    di = feat * n_head
    me = lax.axis_index("seq")
    me_head = lax.axis_index("head")
    first = me == 0
    last = me == n_seq - 1

    def rows(b):
        return pl.ds(pl.multiple_of(b * GROUP, GROUP), GROUP)

    def rows_in(b):
        return pl.ds(pl.multiple_of(b * GROUP + HALO, HALO), GROUP)

    step_copy = pltpu.make_async_copy(step_hbm, stepin, in_sem.at[0])
    bc_copy = pltpu.make_async_copy(bc_hbm.at[0], bcin.at[pl.ds(HALO, length)], in_sem.at[1])

    def x_copy(b):
        return pltpu.make_async_copy(x_hbm.at[0, rows(b)], xin.at[rows_in(b)], in_sem.at[2 + b])

    gate_copy = pltpu.make_async_copy(gate_hbm.at[0], gate, in_sem.at[2 + groups])
    step_copy.start()
    bc_copy.start()
    for b in range(groups):
        x_copy(b).start()
    gate_copy.start()

    barrier = pltpu.get_barrier_semaphore()

    @pl.when(jnp.logical_not(first))
    def _():
        pl.semaphore_signal(barrier, inc=1, device_id={"seq": me - 1}, device_id_type=MESH)

    @pl.when(jnp.logical_not(last))
    def _():
        pl.semaphore_signal(barrier, inc=1, device_id={"seq": me + 1}, device_id_type=MESH)

    def mate(r):
        return lax.rem(me_head + r, n_head)

    for r in range(1, n_head):
        pl.semaphore_signal(barrier, inc=1, device_id={"head": mate(r)}, device_id_type=MESH)

    k_of = lax.rem(lax.broadcasted_iota(jnp.int32, (LANE, feat), 0), 64)
    h_of = lax.broadcasted_iota(jnp.int32, (LANE, feat), 1) // HEADDIM
    expand[...] = jnp.where(k_of == h_of, 1.0, 0.0).astype(BF16)
    dsk[...] = mm(
        split_pair(jnp.broadcast_to(pad_lanes(dskip_ref[...]), (8, LANE))), expand[...]
    )

    peers = n_head - 1 + jnp.where(first, 0, 1) + jnp.where(last, 0, 1)
    pl.semaphore_wait(barrier, peers)

    halo_x = pltpu.make_async_remote_copy(
        src_ref=x_hbm.at[0, pl.ds(length - HALO, HALO)],
        dst_ref=xin.at[pl.ds(0, HALO)],
        send_sem=halo_send.at[0],
        recv_sem=halo_recv.at[0],
        device_id={"seq": me + 1},
        device_id_type=MESH,
    )
    halo_bc = pltpu.make_async_remote_copy(
        src_ref=bc_hbm.at[0, pl.ds(length - HALO, HALO)],
        dst_ref=bcin.at[pl.ds(0, HALO)],
        send_sem=halo_send.at[1],
        recv_sem=halo_recv.at[1],
        device_id={"seq": me + 1},
        device_id_type=MESH,
    )

    @pl.when(jnp.logical_not(last))
    def _():
        halo_x.start()
        halo_bc.start()

    @pl.when(first)
    def _():
        xin[0:HALO, :] = jnp.zeros((HALO, feat), BF16)
        bcin[0:HALO, :] = jnp.zeros((HALO, 2 * STATE), BF16)
        rx[...] = jnp.zeros(rx.shape, BF16)

    step_copy.wait()
    dt_col = to_column(dt_ref[...])
    rate_col = to_column(-LOG2E * jnp.exp(alog_ref[...]))
    upto = (
        lax.broadcasted_iota(jnp.int32, (GROUP, GROUP), 0)
        <= lax.broadcasted_iota(jnp.int32, (GROUP, GROUP), 1)
    )
    upto_ones = jnp.where(upto, 1.0, 0.0).astype(BF16)
    ldt[...] = jnp.zeros(ldt.shape, F32)
    stept[...] = jnp.zeros(stept.shape, F32)

    def decay_body(b, carry):
        v = stepin[:, :, rows(b)].reshape(heads, GROUP) + dt_col[:heads]
        size = jnp.maximum(v, 0.0) + jnp.log1p(jnp.exp(-jnp.abs(v)))
        rate = rate_col[:heads] * size
        hi = rate.astype(BF16)
        rest = rate - hi.astype(F32)
        mid = rest.astype(BF16)
        low = (rest - mid.astype(F32)).astype(BF16)
        total = mm(hi, upto_ones) + mm(mid, upto_ones) + mm(low, upto_ones)
        ldt[b, 0:heads, :] = total
        stept[b, 0:heads, :] = size
        ld[rows(b), :] = ldt[b].T
        step[rows(b), :] = stept[b].T
        return carry

    lax.fori_loop(0, groups, decay_body, 0)
    bc_copy.wait()

    def conv(slot, src, start, cols, taps, at):
        ext[slot] = src[pl.ds(pl.multiple_of(start, HALO), GROUP + HALO), cols].astype(F32)
        total = taps[CONV : CONV + 1, at]
        for k in range(CONV):
            total = total + taps[k : k + 1, at] * ext[slot, pl.ds(HALO - CONV + 1 + k, GROUP), :]
        return silu(total)

    xtap[0:CONV, :] = wx_ref[...].astype(F32)
    xtap[CONV : CONV + 1, :] = bx_ref[...].astype(F32)[None]
    btap[0:CONV, :] = wbc_ref[...].astype(F32)
    btap[CONV : CONV + 1, :] = bbc_ref[...].astype(F32)[None]

    def bc_body(i, carry):
        b = lax.rem(i + 1, groups)

        @pl.when(jnp.logical_and(b == 0, jnp.logical_not(first)))
        def _():
            halo_bc.wait_recv()

        start = b * GROUP
        lanes_b, lanes_c = slice(0, STATE), slice(STATE, 2 * STATE)
        b_part = conv(0, bcin, start, lanes_b, btap, lanes_b).astype(BF16)
        bcc[rows(b), 0:STATE] = b_part
        bcc[rows(b), STATE : 2 * STATE] = conv(1, bcin, start, lanes_c, btap, lanes_c).astype(BF16)
        bt[b] = b_part.astype(F32).T.astype(BF16)
        ld_b = ld[rows(b), :]
        end = ld_b[GROUP - 1 : GROUP]
        tail[rows(b), :] = split_pair(jnp.exp2(end - ld_b) * step[rows(b), :])
        gd[b] = mm(split_pair(jnp.broadcast_to(jnp.exp2(end), (8, LANE))), expand[...])
        return carry

    lax.fori_loop(0, groups, bc_body, 0)

    def relay_copy(c):
        return pltpu.make_async_remote_copy(
            src_ref=tx.at[c],
            dst_ref=rx.at[c],
            send_sem=tx_sem.at[c],
            recv_sem=rx_sem.at[c],
            device_id={"seq": me + 1},
            device_id_type=MESH,
        )

    x_copy(0).wait()
    per = chunk_w // LANE

    def fresh_body(i, carry):
        c = i // groups
        b = lax.rem(lax.rem(i, groups) + 1, groups)

        @pl.when(jnp.logical_and(c == 0, b > 0))
        def _():
            x_copy(b).wait()

        @pl.when(jnp.logical_and(jnp.logical_and(c == 0, b == 0), jnp.logical_not(first)))
        def _():
            halo_x.wait_recv()

        wide = pl.ds(pl.multiple_of(c * chunk_w, chunk_w), chunk_w)
        for j in range(per):
            cols = pl.ds(pl.multiple_of(c * chunk_w + j * LANE, LANE), LANE)
            v = conv(j, xin, b * GROUP, cols, xtap, cols).astype(BF16)
            xc[rows(b), cols] = v
            weight = mm(tail[rows(b), :], expand[:, cols])
            wtd[:, j * LANE : (j + 1) * LANE] = (weight * v.astype(F32)).astype(BF16)
        fresh[b, :, wide] = mm(bt[b], wtd[...])

        @pl.when(b == 0)
        def _():
            total_state = fresh[0, :, wide]
            total_decay = gd[0, :, wide]
            for g in range(1, groups):
                total_state = gd[g, 0:1, wide] * total_state + fresh[g, :, wide]
                total_decay = total_decay * gd[g, :, wide]
            state[:, wide] = total_state
            decay[:, wide] = total_decay

            @pl.when(jnp.logical_and(first, jnp.logical_not(last)))
            def _():
                tx[c] = total_state.astype(BF16)
                relay_copy(c).start()

        return carry

    lax.fori_loop(0, groups * n_chunk, fresh_body, 0)

    def relay(c):
        relay_copy(c).wait_recv()

        @pl.when(jnp.logical_not(last))
        def _():
            cols = pl.ds(pl.multiple_of(c * chunk_w, chunk_w), chunk_w)
            tx[c] = (decay[0:1, cols] * rx[c].astype(F32) + state[:, cols]).astype(BF16)
            relay_copy(c).start()

    points = 2
    events = points * groups

    def relay_event(c):
        near = min(max(2 * c - 3, 0), events - 1)
        second = events - 3 + 2 * c if c < 2 else events + min(c - 1, n_chunk - 3)
        return jnp.where(me == 1, near, jnp.where(me == 2, max(second, 0), events + c))

    def relay_at(e):
        for c in range(n_chunk):

            @pl.when(jnp.logical_and(jnp.logical_not(first), relay_event(c) == e))
            def _():
                relay(c)

    half = GROUP // 2
    low_mask = jnp.where(
        lax.broadcasted_iota(jnp.int32, (1, LANE), 1) < HEADDIM, 1.0, 0.0
    ).astype(BF16)
    high_mask = (1.0 - low_mask.astype(F32)).astype(BF16)
    marks = [(q + 1) * tiles // points - 1 for q in range(points)]

    def intra_body(b, carry):
        inter[...] = mm(bcc[rows(b), STATE : 2 * STATE], bt[b])
        tri_half = (
            lax.broadcasted_iota(jnp.int32, (half, half), 0)
            >= lax.broadcasted_iota(jnp.int32, (half, half), 1)
        )
        for j in range(tiles):
            lo = j * LANE
            x_pair = xc[rows(b), lo : lo + LANE]
            parts = []
            for e in range(2):
                h = 2 * j + e
                x_own = x_pair * (low_mask if e == 0 else high_mask)
                col = ld[rows(b), h : h + 1]
                row = ldt[b, h : h + 1, :]
                size = stept[b, h : h + 1, :]
                quad = {}
                for ti, si in ((0, 0), (1, 0), (1, 1)):
                    ts, sl = slice(ti * half, (ti + 1) * half), slice(si * half, (si + 1) * half)
                    m = inter[ts, sl] * jnp.exp2(col[ts] - row[:, sl]) * size[:, sl]
                    if ti == si:
                        m = jnp.where(tri_half, m, 0.0)
                    quad[ti, si] = m.astype(BF16)
                top = mm(quad[0, 0], x_own[:half])
                bottom = mm(jnp.concatenate((quad[1, 0], quad[1, 1]), axis=1), x_own)
                parts.append((top, bottom))
            skip = dsk[0:1, lo : lo + LANE]
            for ti in range(2):
                at = pl.ds(pl.multiple_of(b * GROUP + ti * half, half), half)
                y[at, lo : lo + LANE] = (
                    parts[0][ti]
                    + parts[1][ti]
                    + skip * x_pair[ti * half : (ti + 1) * half].astype(F32)
                )
            if j in marks:
                relay_at(b * points + marks.index(j))

        return carry

    lax.fori_loop(0, groups, intra_body, 0)
    gate_copy.wait()

    def ss_copy(r):
        return pltpu.make_async_remote_copy(
            src_ref=ss_tx,
            dst_ref=ss_rx.at[r],
            send_sem=ss_send.at[r],
            recv_sem=ss_recv.at[r],
            device_id={"head": mate(r)},
            device_id_type=MESH,
        )

    acc[...] = jnp.zeros(acc.shape, F32)

    def entry_body(b, carry):
        tail[rows(b), :] = split_pair(jnp.exp2(ld[rows(b), :]))
        return carry

    lax.fori_loop(0, groups, entry_body, 0)

    def gate_body(c, carry):
        wide = pl.ds(pl.multiple_of(c * chunk_w, chunk_w), chunk_w)
        relay_at(events + c)
        now = rx[c].astype(F32)
        for b in range(groups):
            at = slice(b * GROUP, (b + 1) * GROUP)
            hi = now.astype(BF16)
            both = jnp.concatenate((hi, (now - hi.astype(F32)).astype(BF16)), axis=0)
            if b < groups - 1:
                now = gd[b, 0:1, wide] * now + fresh[b, :, wide]
            c_part = bcc[at, STATE : 2 * STATE]
            carried = mm(jnp.concatenate((c_part, c_part), axis=1), both)
            scale = mm(tail[at, :], expand[:, wide])
            squares = acc[at, :]
            for j in range(per):
                part = slice(j * LANE, (j + 1) * LANE)
                cols = pl.ds(pl.multiple_of(c * chunk_w + j * LANE, LANE), LANE)
                z = y[at, cols] + scale[:, part] * carried[:, part]
                z = z * silu(gate[at, cols].astype(F32))
                y[at, cols] = z
                squares = squares + z * z
            acc[at, :] = squares
        return carry

    lax.fori_loop(0, n_chunk, gate_body, 0)

    for b in range(groups):
        sums = jnp.sum(acc[b * GROUP : (b + 1) * GROUP, :].T, axis=0, keepdims=True)
        ss_tx[b] = jnp.broadcast_to(sums, (8, GROUP))
    for r in range(1, n_head):
        ss_copy(r).start()
    for r in range(1, n_head):
        ss_copy(r).wait_recv()
    for b in range(groups):
        sums = ss_tx[b]
        for r in range(1, n_head):
            sums = sums + ss_rx[r, b]
        sums_out[b] = sums
    for r in range(1, n_head):
        ss_copy(r).wait_send()

    @pl.when(jnp.logical_not(last))
    def _():
        halo_x.wait_send()
        halo_bc.wait_send()
        for c in range(n_chunk):
            relay_copy(c).wait_send()


def norm_kernel(di, y, sums, gain_ref, out):
    feat = out.shape[2]
    scale = lax.rsqrt(sums[0, 0:1] * (1.0 / di) + norm_eps)
    scale = jnp.broadcast_to(scale, (LANE, GROUP)).T
    at = pl.ds(pl.multiple_of(pl.program_id(0) * GROUP, GROUP), GROUP)
    for j in range(feat // LANE):
        cols = slice(j * LANE, (j + 1) * LANE)
        out[0, :, cols] = (y[at, cols] * scale * gain_ref[cols][None]).astype(BF16)


def on_device(
    x_raw,
    bc_raw,
    gate_in,
    step_raw,
    conv_x_weight,
    conv_x_bias,
    conv_bc_weight,
    conv_bc_bias,
    dt_bias,
    a_log,
    d_skip,
    norm_gain,
):
    length, feat = x_raw.shape[1], x_raw.shape[2]
    heads = dt_bias.shape[0]
    groups = length // GROUP
    tiles = feat // LANE
    n_seq, n_head = lax.axis_size("seq"), lax.axis_size("head")
    n_chunk = tiles // 2 if tiles % 2 == 0 else tiles
    chunk_w = feat // n_chunk
    anyspec = pl.BlockSpec(memory_space=pl.ANY)
    vspec = pl.BlockSpec(memory_space=pltpu.VMEM)
    V = pltpu.VMEM
    DMA = pltpu.SemaphoreType.DMA
    vmem_limit = 67043328 - length * feat * 4 - (128 << 10)
    call = pl.pallas_call(
        functools.partial(kernel, n_seq, n_head),
        out_shape=(V((length, feat), F32), jax.ShapeDtypeStruct((groups, 8, GROUP), F32)),
        in_specs=[anyspec] * 4 + [vspec] * 7,
        out_specs=(vspec, vspec),
        scratch_shapes=[
            V((HALO + length, feat), BF16),
            V((HALO + length, 2 * STATE), BF16),
            V((length, feat), BF16),
            V((heads, 1, length), F32),
            V((length, feat), BF16),
            V((length, 2 * STATE), BF16),
            V((groups, STATE, GROUP), BF16),
            V((length, LANE), F32),
            V((length, LANE), F32),
            V((groups, LANE, GROUP), F32),
            V((groups, LANE, GROUP), F32),
            V((2, GROUP + HALO, LANE), F32),
            V((8, feat), F32),
            V((8, 2 * STATE), F32),
            V((length, LANE), BF16),
            V((length, LANE), F32),
            V((LANE, feat), BF16),
            V((GROUP, chunk_w), BF16),
            V((groups, STATE, feat), F32),
            V((groups, 8, feat), F32),
            V((STATE, feat), F32),
            V((8, feat), F32),
            V((8, feat), F32),
            V((GROUP, GROUP), F32),
            V((n_chunk, STATE, chunk_w), BF16),
            V((n_chunk, STATE, chunk_w), BF16),
            V((groups, 8, GROUP), F32),
            V((n_head, groups, 8, GROUP), F32),
            DMA((3 + groups,)),
            DMA((2,)),
            DMA((2,)),
            DMA((n_chunk,)),
            DMA((n_chunk,)),
            DMA((n_head,)),
            DMA((n_head,)),
        ],
        compiler_params=pltpu.CompilerParams(
            collective_id=0, has_side_effects=True, vmem_limit_bytes=vmem_limit
        ),
        name="ssd_layer",
    )
    gated, sums = call(
        x_raw,
        bc_raw,
        gate_in,
        jnp.transpose(step_raw, (2, 0, 1)),
        conv_x_weight,
        conv_x_bias,
        conv_bc_weight,
        conv_bc_bias,
        dt_bias[None],
        a_log[None],
        d_skip[None],
    )
    return pl.pallas_call(
        functools.partial(norm_kernel, feat * n_head),
        grid=(groups,),
        out_shape=jax.ShapeDtypeStruct(x_raw.shape, BF16),
        in_specs=[vspec, pl.BlockSpec((1, 8, GROUP), lambda i: (i, 0, 0)), vspec],
        out_specs=pl.BlockSpec((1, GROUP, feat), lambda i: (0, i, 0)),
        compiler_params=pltpu.CompilerParams(vmem_limit_bytes=16 << 20),
        name="norm",
    )(gated, sums, norm_gain)


def solution(mesh):
    in_specs = (
        P(("member", "rep"), "seq", "head"),
        P(("member", "rep"), "seq", None),
        P(("member", "rep"), "seq", "head"),
        P(("member", "rep"), "seq", "head"),
        P("member", "head"),
        P(("member", "head")),
        P("member", None),
        P("member"),
        P(("member", "head")),
        P(("member", "head")),
        P(("member", "head")),
        P(("member", "head")),
    )
    out_specs = P(("member", "rep"), "seq", "head")
    return jax.shard_map(
        on_device, mesh=mesh, in_specs=in_specs, out_specs=out_specs, check_vma=False
    )
```

time: 44.8 us -> 34.7 us (0.77)
  local copies, waits for them, and re-layouts: 9.12 us -> 0.75 us
  Pallas kernels: 35.4 us -> 33.7 us
    unnamed x2 -> x4, local copies, waits for them, and re-layouts: 5.3 us -> 0.75 us
    broadcast_in_dim x3 -> x0, local copies, waits for them, and re-layouts: 3.82 us -> none  [the longest x1 1.29 us: on_device(): norm_gain[None]]
    pallas_call x1 -> x2, Pallas kernels: 35.4 us -> 33.7 us  [the longest x1 31.3 us: on_device(): call(x_raw, bc_raw, gate_in, jnp.transpose(step_raw, (2, 0, 1)), conv_x_w...]
where the time goes in v2:
time: 34.7 us; the launch traced here: 34.4 us
  Pallas kernels  33.7 us (97%)
  local copies, waits for them, and re-layouts  0.75 us (2%)
    pallas_call x1, Pallas kernels, on_device(): call(x_raw, bc_raw, gate_in, jnp.transpose(step_raw, (2, 0, 1)), conv_x_w...  31.3 us
    pallas_call x1, Pallas kernels, on_device(): pl.pallas_call(functools.partial(norm_kernel, feat * n_head), grid=(group...  2.37 us
    unnamed x4, local copies, waits for them, and re-layouts  0.75 us

profile of v2, /device:TPU:24, one launch (start us, length us, event | category | flops | bytes accessed | tf_op | source)
XLA Modules:
  0.0 34.4 jit_solution(17073966922812190293)
XLA Ops:
  0.0 0.0 copy-start.1
  0.0 31.3 %ssd_layer.1 = (f32[1024,1280]{1,0:T(8,128)S(1)}, f32[4,8,256]{2,1,0:T(8,128)}) custom-call(bf16[1,1024,1280]{2,1,0:T(8,128)(2,1)} %x_hbm.1, bf16[1,1024,256]{2,1,0:T(8,128)(2,1)} %bc_hbm.1, bf16[1,1024,1280]{2,1,0:T(8,128)(2,1)} %gate_hbm.1, f32[20,1,1024]{2,1,0:T(1,128)} %bitcast.4, bf16[4,1280]{1,0:T(4,128)(2,1)} %wx_ref.1, bf16[1280]{0:T(1024)(128)(2,1)} %bx_ref.1, ...), custom_call_target="tpu_custom_call" | custom-call | tf_op jit(solution)/shard_map/ssd_layer/pallas_call | solution.py:523
  31.3 0.0 copy-done.1
  31.3 0.0 copy-start
  31.3 0.7 %copy-done = f32[4,8,256]{2,1,0:T(8,128)S(1)} copy-done((f32[4,8,256]{2,1,0:T(8,128)S(1)}, f32[4,8,256]{2,1,0:T(8,128)}, u32[]{:S(2)}) %copy-start) | copy-done | bytes 32792
  32.1 2.4 %norm.1 = bf16[1,1024,1280]{2,1,0:T(8,128)(2,1)} custom-call(f32[1024,1280]{1,0:T(8,128)S(1)} %get-tuple-element.7.y, f32[4,8,256]{2,1,0:T(8,128)S(1)} %copy-done, f32[1280]{0:T(1024)S(1)} %copy-done.1), custom_call_target="tpu_custom_call" | custom-call | tf_op jit(solution)/shard_map/norm/pallas_call | solution.py:536
Async XLA Ops:
  0.0 31.3 %copy-start.1 = (f32[1280]{0:T(1024)S(1)}, f32[1280]{0:T(1024)}, u32[]{:S(2)}) copy-start(f32[1280]{0:T(1024)} %gain_ref.1) | copy-start | bytes 15364
  31.3 0.8 %copy-start = (f32[4,8,256]{2,1,0:T(8,128)S(1)}, f32[4,8,256]{2,1,0:T(8,128)}, u32[]{:S(2)}) copy-start(f32[4,8,256]{2,1,0:T(8,128)} %get-tuple-element.8.sums) | copy-start | bytes 98308
